TPU v7x, 256 devices: a 4x2x16 block of a 4x16x16 slice. The times are simulated.
256 devices in a mesh: group: 2 (over y), pages: 16 (over z), heads: 8 (over x, core).
Axes of the slice: x: 4, y: 2, z: 16, core: 2. Of those that a mesh axis runs over, the one named last changes fastest.
The devices are a block of a 4x16x16 slice.
Arguments:
- queries: bfloat16 [32, 48, 128], P('group', 'heads'), parts along dimension 0, may hold values from -180 to 180
- k_cache: bfloat16 [8, 32768, 16, 128], P('heads', ('group', 'pages')), parts along dimension 1, may hold values from -6 to 6
- v_cache: bfloat16 [8, 32768, 16, 128], P('heads', ('group', 'pages')), parts along dimension 1, may hold values from -6 to 6
- new_key: bfloat16 [8, 32, 128], P('heads', 'group'), parts along dimension 1, may hold values from -6 to 6
- new_value: bfloat16 [8, 32, 128], P('heads', 'group'), parts along dimension 1, may hold values from -6 to 6
- ctx_lens: int32 [32], P('group'), parts along dimension 0, may hold values from 4081 to 16384, as said below
- page_owner: int32 [32, 1024], P('group'), parts along dimension 0, may hold values from -1 to 15, as said below
- page_slot: int32 [32, 1024], P('group'), parts along dimension 0, may hold values from 0 to 1023, as said below
- out_weight: bfloat16 [6144, 6144], P(None, 'pages'), may hold values from -0.078125 to 0.078125
Outputs:
- projected: bfloat16 [32, 6144], P(('group', 'heads'), 'pages'), parts along dimension 0
There are 2 independent parts, one for each index of `group`. A program takes and returns all parts, laid end to end along the dimension named above; an argument that names none is the same for every part. Nothing has to cross between parts.
Inputs may be any that keep to these rules, and one draw needn't show every extreme that they name: Request r holds ceil(ctx_lens[r] / 16) pages; some request holds 16384 tokens. `page_owner`: for j below request r's page count, the device along pages that holds its logical page j; -1 beyond. No two live pages share a device and a slot. `page_slot`: for j below request r's page count, the slot of logical page j on its device; 0 beyond.
All inputs are finite; a program needn't handle non-finite values.
Results may differ from a plain program's by a relative error of at most 0.0053.
Values may be sent and summed in bfloat16 or wider, within the bound.
No kernel may reach another device: no remote copies, remote signals or barrier semaphores. Data moves between devices by JAX's collectives and lax.ppermute only.
A program may use at most 64 MiB of HBM per device.

v0:
```python
import math

import jax
import jax.numpy as jnp
from jax import lax
from jax.sharding import Mesh
from jax.sharding import PartitionSpec as P

HEADS = ("heads_0", "heads_1")
GROUP_HEADS = ("group", "heads_0", "heads_1")


very_low = -1e30
highest = lax.Precision.HIGHEST


def gathered_once(x, axis):
    leaves = jax.tree.leaves(x)
    order = sorted(range(len(leaves)), key=lambda k: -leaves[k].size)
    width = (1, *leaves[order[0]].shape)[-1]
    lines = [
        jnp.pad(leaves[k].reshape(-1), (0, -leaves[k].size % width)).reshape(-1, width)
        for k in order
    ]
    both, at, found = (lax.all_gather(jnp.concatenate(lines), axis), 0, {})
    for k, line in zip(order, lines):
        slab = both[:, at : at + len(line)].reshape(len(both), -1)
        found[k] = slab[:, : leaves[k].size].reshape(-1, *leaves[k].shape)
        at += len(line)
    numbers = iter(range(len(leaves)))
    return jax.tree.map(lambda _: found[next(numbers)], x)


def merged(x, axis, combine):
    everything = gathered_once(x, axis)
    leading = jax.tree.map(lambda part: part[0], everything)

    def turn(k, so_far):
        return combine(so_far, jax.tree.map(lambda part: part[k], everything))

    return lax.fori_loop(1, lax.axis_size(axis), turn, leading)


def cut_along(x, dim, peers):
    lengths = x.shape
    blocks = x.reshape(*lengths[:dim], peers, lengths[dim] // peers, *lengths[dim + 1 :])
    return jnp.moveaxis(blocks, dim, 0)


def laid_out(blocks, dim):
    blocks = jnp.moveaxis(blocks, 0, dim)
    lengths = blocks.shape
    return blocks.reshape(*lengths[:dim], lengths[dim] * lengths[dim + 1], *lengths[dim + 2 :])


def exchange_in_order(blocks, axes, order):
    inside = blocks.shape[1:]
    result = blocks.reshape(*(lax.axis_size(a) for a in axes), *inside)
    for k in order:
        result = lax.all_to_all(result, axes[k], k, k, tiled=True)
    return result.reshape(-1, *inside)


def two_step_exchange(x, groups, order, split_dim, concat_dim):
    peers = lax.axis_size(groups[0]) * lax.axis_size(groups[1])
    blocks = cut_along(x, split_dim, peers)
    return laid_out(exchange_in_order(blocks, groups, order), concat_dim)


def softmax_combine(first_part, second_part):
    first_top, first_out, first_sum = first_part
    second_top, second_out, second_sum = second_part
    peak_score = jnp.maximum(first_top, second_top)
    first_factor = jnp.exp(first_top - peak_score)
    second_factor = jnp.exp(second_top - peak_score)
    partial_out = first_out * first_factor[..., None] + second_out * second_factor[..., None]
    weight_sum = first_sum * first_factor + second_sum * second_factor
    return (peak_score, partial_out, weight_sum)


def combine_pages(peak_score, partial_out, weight_sum):
    return merged((peak_score, partial_out, weight_sum), "pages", softmax_combine)


def finish(peak_score, partial_out, weight_sum, self_score, self_value, group_size):
    expanded = jnp.repeat(self_value, group_size, axis=1)
    peak_value = jnp.maximum(peak_score, self_score)
    keep_old = jnp.exp(peak_score - peak_value)
    take_new = jnp.exp(self_score - peak_value)
    attended = (partial_out * keep_old[..., None] + expanded * take_new[..., None]) / (
        weight_sum * keep_old + take_new
    )[..., None]
    return attended.astype(jnp.bfloat16)


def slot_tables(target, entry_request, entry_page, entry_length, slot_count):
    block_size = math.gcd(slot_count, 128)
    block_count = slot_count // block_size

    def one_block(block_number):
        slot_numbers = block_number * block_size + jnp.arange(block_size, dtype=jnp.int32)
        matched = target[None, :] == slot_numbers[:, None]
        owner = jnp.max(jnp.where(matched, entry_request[None, :], -1), axis=1)
        page_number = jnp.max(jnp.where(matched, entry_page[None, :], 0), axis=1)
        length = jnp.max(jnp.where(matched, entry_length[None, :], 0), axis=1)
        return (owner, page_number, length)

    owners, pages_found, lengths_found = lax.map(
        one_block, jnp.arange(block_count, dtype=jnp.int32)
    )
    return (
        owners.reshape(slot_count),
        pages_found.reshape(slot_count),
        lengths_found.reshape(slot_count),
    )


def local(
    queries, k_cache, v_cache, new_key, new_value, ctx_lens, page_owner, page_slot, out_weight
):
    kv_local, slot_count, page_rows, head_dim = k_cache.shape
    requests, q_local, _ = queries.shape
    group_size = q_local // kv_local
    max_pages = page_owner.shape[1]
    scaling = 1.0 / math.sqrt(head_dim)
    page_index = lax.axis_index("pages")
    request_ids = jnp.broadcast_to(jnp.arange(requests, dtype=jnp.int32)[:, None], page_owner.shape)
    page_ids = jnp.broadcast_to(jnp.arange(max_pages, dtype=jnp.int32)[None, :], page_owner.shape)
    entry_length = jnp.broadcast_to(ctx_lens[:, None], page_owner.shape)
    target = jnp.where(page_owner == page_index, page_slot, slot_count).reshape(-1)
    slot_request, slot_page, slot_length = slot_tables(
        target, request_ids.reshape(-1), page_ids.reshape(-1), entry_length.reshape(-1), slot_count
    )
    position = slot_page[:, None] * page_rows + jnp.arange(page_rows, dtype=jnp.int32)[None, :]
    live_mask = (position < slot_length[:, None])[:, None, None, :]
    belongs = slot_request[None, :] == jnp.arange(requests, dtype=jnp.int32)[:, None]
    belongs_low = belongs.astype(jnp.bfloat16)
    slot_query = (
        jnp.dot(
            belongs_low.T,
            queries.reshape(requests, q_local * head_dim),
            preferred_element_type=jnp.float32,
        )
        .astype(jnp.bfloat16)
        .reshape(slot_count, kv_local, group_size, head_dim)
    )
    grouped = queries.reshape(requests, kv_local, group_size, head_dim)
    scores = (
        jnp.einsum("pkgd,kptd->pkgt", slot_query, k_cache, preferred_element_type=jnp.float32)
        * scaling
    )
    scores = jnp.where(live_mask, scores, very_low)
    page_top = jnp.max(scores, axis=3)
    weights = jnp.where(live_mask, jnp.exp(scores - page_top[..., None]), 0.0)
    page_total = jnp.sum(weights, axis=3)
    page_out = jnp.einsum(
        "pkgt,kptd->pkgd", weights.astype(jnp.bfloat16), v_cache, preferred_element_type=jnp.float32
    )
    flat_top = page_top.reshape(slot_count, q_local)
    device_top = jnp.max(jnp.where(belongs[:, :, None], flat_top[None, :, :], very_low), axis=1)
    slot_top = jnp.max(jnp.where(belongs[:, :, None], device_top[:, None, :], very_low), axis=0)
    factor = jnp.exp(flat_top - slot_top)
    scaled = page_out.reshape(slot_count, q_local * head_dim) * jnp.repeat(factor, head_dim, axis=1)
    belongs_float = belongs.astype(jnp.float32)
    device_out = jnp.dot(
        belongs_float, scaled, precision=highest, preferred_element_type=jnp.float32
    ).reshape(requests, q_local, head_dim)
    device_sum = jnp.dot(
        belongs_float,
        page_total.reshape(slot_count, q_local) * factor,
        precision=highest,
        preferred_element_type=jnp.float32,
    )
    self_score = (
        jnp.einsum("rkgd,krd->rkg", grouped, new_key, preferred_element_type=jnp.float32).reshape(
            requests, q_local
        )
        * scaling
    )
    self_value = jnp.transpose(new_value, (1, 0, 2)).astype(jnp.float32)
    peak_score, partial_out, weight_sum = combine_pages(device_top, device_out, device_sum)
    attended = finish(peak_score, partial_out, weight_sum, self_score, self_value, group_size)
    head_rows = two_step_exchange(attended, ("heads_0", "heads_1"), (1, 0), 0, 1)
    flat_rows = head_rows.reshape(head_rows.shape[0], head_rows.shape[1] * head_rows.shape[2])
    return jnp.dot(flat_rows, out_weight, preferred_element_type=jnp.float32).astype(jnp.bfloat16)


def solution(mesh):
    torus = Mesh(
        mesh.devices.reshape(mesh.shape["group"], mesh.shape["pages"], 4, 2),
        ("group", "pages", "heads_0", "heads_1"),
    )
    in_specs = (
        P("group", HEADS, None),
        P(HEADS, ("group", "pages"), None, None),
        P(HEADS, ("group", "pages"), None, None),
        P(HEADS, "group", None),
        P(HEADS, "group", None),
        P("group"),
        P("group", None),
        P("group", None),
        P(None, "pages"),
    )
    out_specs = P(GROUP_HEADS, "pages")
    return jax.shard_map(local, mesh=torus, in_specs=in_specs, out_specs=out_specs, check_vma=False)
```

profile of v0, /device:TPU:40, one launch (start us, length us, event | category | flops | bytes accessed | tf_op | source)
XLA Modules:
  0.0 171.8 jit_solution(7054935056416315920)
XLA Ops:
  0.0 0.9 compare_select_fusion.3
  0.9 51.7 %while.35 = (s32[]{:T(128)}, s32[8,128]{1,0:T(8,128)S(1)}, s32[8,128]{1,0:T(8,128)S(1)}, s32[8,128]{1,0:T(8,128)S(1)}, s32[16,1024]{1,0:T(8,128)S(1)}, /*index=5...) while((s32[]{:T(128)}, s32[8,128]{1,0:T(8,128)S(1)}, s32[8,128]{1,0:T(8,128)S(1)}, ...), condition=%wide.region_4.5_spmd.clone, body=%wide.region_0.4_spmd.clone.sunk | while | flops 14679811 | bytes 988877 | solution.py:108
  2.3 0.7 broadcast_bitcast_fusion.2
  3.2 4.1 %fusion.59 = (s32[128]{0:T(128)S(1)}, s32[128]{0:T(128)S(1)}, s32[128]{0:T(128)S(1)}) fusion(s32[16384]{0:T(1024)S(1)} %bitcast.118, s32[16384]{0:T(1024)S(1)} %bitcast.119, s32[128]{0:T(128)S(1)} %iota_add_fusion.2, s32[16384]{0:T(1024)S(1)} %bitcast.120, s32[16384]{0:T(1024)S(1)} %bitcast.121), kind=kLoop, calls=%fused_computation.18.clone.1 | loop fusion | flops 14679680 | bytes 264192 | tf_op jit(solution)/shard_map/while/body/eval_jaxpr/reduce_max | solution.py:105
  8.8 0.7 broadcast_bitcast_fusion.2
  9.6 4.1 %fusion.59 = (s32[128]{0:T(128)S(1)}, s32[128]{0:T(128)S(1)}, s32[128]{0:T(128)S(1)}) fusion(s32[16384]{0:T(1024)S(1)} %bitcast.118, s32[16384]{0:T(1024)S(1)} %bitcast.119, s32[128]{0:T(128)S(1)} %iota_add_fusion.2, s32[16384]{0:T(1024)S(1)} %bitcast.120, s32[16384]{0:T(1024)S(1)} %bitcast.121), kind=kLoop, calls=%fused_computation.18.clone.1 | loop fusion | flops 14679680 | bytes 264192 | tf_op jit(solution)/shard_map/while/body/eval_jaxpr/reduce_max | solution.py:105
  16.1 4.1 %fusion.59 = (s32[128]{0:T(128)S(1)}, s32[128]{0:T(128)S(1)}, s32[128]{0:T(128)S(1)}) fusion(s32[16384]{0:T(1024)S(1)} %bitcast.118, s32[16384]{0:T(1024)S(1)} %bitcast.119, s32[128]{0:T(128)S(1)} %iota_add_fusion.2, s32[16384]{0:T(1024)S(1)} %bitcast.120, s32[16384]{0:T(1024)S(1)} %bitcast.121), kind=kLoop, calls=%fused_computation.18.clone.1 | loop fusion | flops 14679680 | bytes 264192 | tf_op jit(solution)/shard_map/while/body/eval_jaxpr/reduce_max | solution.py:105
  22.6 4.1 %fusion.59 = (s32[128]{0:T(128)S(1)}, s32[128]{0:T(128)S(1)}, s32[128]{0:T(128)S(1)}) fusion(s32[16384]{0:T(1024)S(1)} %bitcast.118, s32[16384]{0:T(1024)S(1)} %bitcast.119, s32[128]{0:T(128)S(1)} %iota_add_fusion.2, s32[16384]{0:T(1024)S(1)} %bitcast.120, s32[16384]{0:T(1024)S(1)} %bitcast.121), kind=kLoop, calls=%fused_computation.18.clone.1 | loop fusion | flops 14679680 | bytes 264192 | tf_op jit(solution)/shard_map/while/body/eval_jaxpr/reduce_max | solution.py:105
  29.0 4.1 %fusion.59 = (s32[128]{0:T(128)S(1)}, s32[128]{0:T(128)S(1)}, s32[128]{0:T(128)S(1)}) fusion(s32[16384]{0:T(1024)S(1)} %bitcast.118, s32[16384]{0:T(1024)S(1)} %bitcast.119, s32[128]{0:T(128)S(1)} %iota_add_fusion.2, s32[16384]{0:T(1024)S(1)} %bitcast.120, s32[16384]{0:T(1024)S(1)} %bitcast.121), kind=kLoop, calls=%fused_computation.18.clone.1 | loop fusion | flops 14679680 | bytes 264192 | tf_op jit(solution)/shard_map/while/body/eval_jaxpr/reduce_max | solution.py:105
  35.5 4.1 %fusion.59 = (s32[128]{0:T(128)S(1)}, s32[128]{0:T(128)S(1)}, s32[128]{0:T(128)S(1)}) fusion(s32[16384]{0:T(1024)S(1)} %bitcast.118, s32[16384]{0:T(1024)S(1)} %bitcast.119, s32[128]{0:T(128)S(1)} %iota_add_fusion.2, s32[16384]{0:T(1024)S(1)} %bitcast.120, s32[16384]{0:T(1024)S(1)} %bitcast.121), kind=kLoop, calls=%fused_computation.18.clone.1 | loop fusion | flops 14679680 | bytes 264192 | tf_op jit(solution)/shard_map/while/body/eval_jaxpr/reduce_max | solution.py:105
  42.0 4.1 %fusion.59 = (s32[128]{0:T(128)S(1)}, s32[128]{0:T(128)S(1)}, s32[128]{0:T(128)S(1)}) fusion(s32[16384]{0:T(1024)S(1)} %bitcast.118, s32[16384]{0:T(1024)S(1)} %bitcast.119, s32[128]{0:T(128)S(1)} %iota_add_fusion.2, s32[16384]{0:T(1024)S(1)} %bitcast.120, s32[16384]{0:T(1024)S(1)} %bitcast.121), kind=kLoop, calls=%fused_computation.18.clone.1 | loop fusion | flops 14679680 | bytes 264192 | tf_op jit(solution)/shard_map/while/body/eval_jaxpr/reduce_max | solution.py:105
  48.4 4.1 %fusion.59 = (s32[128]{0:T(128)S(1)}, s32[128]{0:T(128)S(1)}, s32[128]{0:T(128)S(1)}) fusion(s32[16384]{0:T(1024)S(1)} %bitcast.118, s32[16384]{0:T(1024)S(1)} %bitcast.119, s32[128]{0:T(128)S(1)} %iota_add_fusion.2, s32[16384]{0:T(1024)S(1)} %bitcast.120, s32[16384]{0:T(1024)S(1)} %bitcast.121), kind=kLoop, calls=%fused_computation.18.clone.1 | loop fusion | flops 14679680 | bytes 264192 | tf_op jit(solution)/shard_map/while/body/eval_jaxpr/reduce_max | solution.py:105
  52.7 1.8 %convolution_convert_fusion = bf16[1024,768]{0,1:T(8,128)(2,1)} fusion(s32[1024]{0:T(1024)S(1)} %bitcast.129, bf16[16,6,128]{2,0,1:T(8,128)(2,1)S(1)} %copy-done.1), kind=kOutput, calls=%fused_computation.38 | convolution fusion | flops 25968640 | bytes 1601536 | tf_op jit(solution)/shard_map/dot_general | solution.py:139
  54.5 3.2 %copy.104 = bf16[1024,6,128]{2,1,0:T(8,128)(2,1)S(1)} copy(bf16[1024,6,128]{0,2,1:T(8,128)(2,1)} %bitcast.122) | data formatting | bytes 3145728 | tf_op jit(solution)/shard_map/reshape.2
  58.1 6.5 %fusion.17 = (f32[1024,6]{1,0:T(8,128)S(1)}, f32[1024,6,16]{2,1,0:T(8,128)}) fusion(pred[1024,16]{1,0:T(8,128)(4,1)S(1)} %add_compare_fusion, bf16[1024,6,128]{2,1,0:T(8,128)(2,1)S(1)} %copy.104, bf16[1,1024,16,128]{3,2,1,0:T(8,128)(2,1)} %param.14), kind=kOutput, calls=%fused_computation.29 | convolution fusion | flops 25454592 | bytes 6201344 | tf_op jit(solution)/shard_map/pkgd,kptd->pkgt/dot_general | solution.py:149
  65.4 15.7 %fusion.18 = f32[1024,6]{1,0:T(8,128)S(1)} fusion(f32[1024,6,16]{2,1,0:T(8,128)} %get-tuple-element.340, f32[1024,6]{1,0:T(8,128)S(1)} %get-tuple-element.339, pred[1024,16]{1,0:T(8,128)(4,1)S(1)} %add_compare_fusion), kind=kLoop, calls=%fused_computation.30 | loop fusion | flops 485376 | bytes 458752 | tf_op jit(solution)/shard_map/reduce_sum | solution.py:155
  81.7 6.6 %fusion.20 = f32[1024,6,128]{2,1,0:T(8,128)} fusion(bf16[1,1024,16,128]{3,2,1,0:T(8,128)(2,1)} %param.15, f32[1024,6,16]{2,1,0:T(8,128)} %get-tuple-element.340, f32[1024,6]{1,0:T(8,128)S(1)} %subtract_exponential_fusion.1, f32[1024,6]{1,0:T(8,128)S(1)} %get-tuple-element.339, pred[1024,16]{1,0:T(8,128)(4,1)S(1)} %add_compare_fusion), kind=kOutput, calls=%fused_computation.32 | convolution fusion | flops 26443776 | bytes 7798784 | tf_op jit(solution)/shard_map/pkgt,kptd->pkgd/dot_general | solution.py:156
  88.3 3.9 %copy.107 = f32[1024,6,128]{0,2,1:T(8,128)S(1)} copy(f32[1024,6,128]{2,1,0:T(8,128)} %fusion.20) | data formatting | bytes 6291456 | tf_op jit(solution)/shard_map/mul | solution.py:163
  92.1 1.5 fusion.31
  93.7 53.1 %all-gather.1 = f32[16,98,128]{2,1,0:T(8,128)S(1)} all-gather(f32[1,98,128]{2,1,0:T(8,128)S(1)} %maximum_bitcast_fusion), channel_id=2, replica_groups=mesh['group'=2,'pages'=16,'heads_0'=4,'heads_1'=2] {'pages'}, dimensions={0}, use_global_device_ids=true | all-gather | bytes 852992 | tf_op jit(solution)/shard_map/all_gather | solution.py:25
  148.4 5.6 %while.34 = (s32[]{:T(128)}, f32[16,6]{0,1:T(8,128)S(1)}, f32[16,6,128]{2,1,0:T(8,128)S(1)}, f32[16,6]{0,1:T(8,128)S(1)}, f32[16,16,6]{1,2,0:T(8,128)S(1)}, /*in...) while((s32[]{:T(128)}, f32[16,6]{0,1:T(8,128)S(1)}, ...), condition=%wide.region_10.11_spmd, body=%wide.region_9.10_spmd.sunk | while | flops 37445 | bytes 251287 | solution.py:41
  154.6 3.8 %all_to_all.10 = bf16[4,2,2,6,128]{4,0,3,2,1:T(4,128)(2,1)S(1)} all-to-all(bf16[4,2,2,6,128]{4,0,3,2,1:T(4,128)(2,1)S(1)} %copy.122), channel_id=1, replica_groups=mesh['group'=2,'pages'=16,'heads_0'=4,'heads_1'=2] {'heads_1'}, dimensions={1} | all-to-all | bytes 49152 | tf_op jit(solution)/shard_map/all_to_all | solution.py:60
  158.4 9.8 %all_to_all.11 = bf16[4,2,2,6,128]{4,2,3,1,0:T(2,128)(2,1)S(1)} all-to-all(bf16[4,2,2,6,128]{4,2,3,1,0:T(2,128)(2,1)S(1)} %copy.123), channel_id=1, replica_groups=mesh['group'=2,'pages'=16,'heads_0'=4,'heads_1'=2] {'heads_0'}, dimensions={0} | all-to-all | bytes 49152 | tf_op jit(solution)/shard_map/all_to_all | solution.py:60
  168.2 3.6 %convolution_convert_fusion.1 = bf16[2,384]{1,0:T(2,128)(2,1)} fusion(bf16[2,6144]{1,0:T(2,128)(2,1)S(1)} %reshape_reshape.12, bf16[6144,384]{1,0:T(8,128)(2,1)} %param.21), kind=kOutput, calls=%fused_computation.39 | convolution fusion | flops 9437952 | bytes 4744704 | tf_op jit(solution)/shard_map/dot_general | solution.py:185
  (221 shorter events, 20.1 us)
Async XLA Ops:
  0.0 153.9 %copy-start = (bf16[1,16,128]{2,1,0:T(8,128)(2,1)S(1)}, bf16[1,16,128]{2,1,0:T(8,128)(2,1)}, u32[]{:S(2)}) copy-start(bf16[1,16,128]{2,1,0:T(8,128)(2,1)} %param.16) | copy-start | bytes 12292
  0.0 52.7 %copy-start.1 = (bf16[16,6,128]{2,0,1:T(8,128)(2,1)S(1)}, bf16[16,6,128]{2,0,1:T(8,128)(2,1)}, u32[]{:S(2)}) copy-start(bf16[16,6,128]{2,0,1:T(8,128)(2,1)} %param.13) | copy-start | bytes 73732
  93.7 60.8 %copy-start.2 = (bf16[1,16,128]{2,1,0:T(8,128)(2,1)S(1)}, bf16[1,16,128]{2,1,0:T(8,128)(2,1)}, u32[]{:S(2)}) copy-start(bf16[1,16,128]{2,1,0:T(8,128)(2,1)} %param.17) | copy-start | bytes 12292
where the time goes:
time: 172 us
  blocking collectives  66.7 us (39%)
  other arithmetic  52.4 us (30%)
  local copies, waits for them, and re-layouts  25.4 us (15%)
  matrix products  20.4 us (12%)
  loops' own time  6.63 us (4%)
    all_gather x1, blocking collectives, gathered_once(): both, at, found = (lax.all_gather(jnp.concatenate(lines), axis), 0, {})  53.1 us
    reduce_max x8, other arithmetic, one_block(): length = jnp.max(jnp.where(matched, entry_length[None, :], 0), axis=1)  33 us
    reduce_sum x1, other arithmetic, local(): page_total = jnp.sum(weights, axis=3)  15.7 us
    all_to_all x2, blocking collectives, exchange_in_order(): result = lax.all_to_all(result, axes[k], k, k, tiled=True)  13.5 us
    dot_general x1, matrix products, local(): jnp.einsum('pkgt,kptd->pkgd', weights.astype(jnp.bfloat16), v_cache, pref...  6.59 us
    dot_general x1, matrix products, local(): jnp.einsum('pkgd,kptd->pkgt', slot_query, k_cache, preferred_element_type...  6.46 us
    while x56, local copies, waits for them, and re-layouts  6.43 us
    another operation x1, loops' own time, slot_tables(): lax.map(one_block, jnp.arange(block_count, dtype=jnp.int32))  6.09 us

commit v1 on v0

v1 whole, which is shorter than its diff:
```python
import math

import jax
import jax.numpy as jnp
from jax import lax
from jax.experimental import pallas as pl
from jax.experimental.pallas import tpu as pltpu
from jax.sharding import Mesh
from jax.sharding import PartitionSpec as P

NEAR = 4
CHUNK = 2048
SIDE = 32
BLOCK = 8
W_CHUNKS = 6

f32 = jnp.float32
bf16 = jnp.bfloat16
masked = -1e30
lowest = -1e29


def iota(shape, dim):
    return lax.broadcasted_iota(jnp.int32, shape, dim)


def dot(a, b):
    return jnp.dot(a, b, preferred_element_type=f32)


def dot_t(a, b):
    return lax.dot_general(a, b, (((1,), (1,)), ((), ())), preferred_element_type=f32)


def split3(x):
    hi = x.astype(bf16).astype(f32)
    mid = (x - hi).astype(bf16).astype(f32)
    lo = (x - hi - mid).astype(bf16).astype(f32)
    return [hi, mid, lo]


def attend_kernel(
    me_ref, lens_ref, owner_ref, slot_ref, q_ref, nk_ref, nv_ref, k_hbm, v_hbm, out_ref,
    k_buf, v_buf, hi_ref, lo_ref, val_ref, key_ref, sems,
):
    requests, max_pages = owner_ref.shape
    rows, dim = q_ref.shape
    heads = rows // requests
    tokens = k_buf.shape[0]
    page = tokens // (SIDE * SIDE)
    steps = tokens // CHUNK
    copies = []
    for c in range(steps):
        part = pl.ds(c * CHUNK, CHUNK)
        pair = (
            pltpu.make_async_copy(k_hbm.at[part], k_buf.at[part], sems.at[0, c]),
            pltpu.make_async_copy(v_hbm.at[part], v_buf.at[part], sems.at[1, c]),
        )
        for copy in pair:
            copy.start()
        copies.append(pair)

    me = me_ref[0]
    row = iota((requests, 128), 0)
    lens = jnp.zeros((requests, 128), jnp.int32)
    for r in range(requests):
        lens = jnp.where(row == r, lens_ref[r], lens)
    lens = jnp.concatenate([lens] * (max_pages // 128), axis=1)
    live = jnp.clip(lens - page * iota(lens.shape, 1), 0, page)
    val = jnp.where(owner_ref[...] == me, iota(lens.shape, 0) * page + live, 0)
    hi_ref[...] = slot_ref[...] >> 5
    lo_ref[...] = slot_ref[...] & 31
    val_ref[...] = val.astype(f32)
    side = iota((SIDE, 128), 0)
    wide = BLOCK * SIDE
    table = jnp.zeros((wide, wide), f32)
    for j in range(max_pages // 128):
        lanes = slice(j * 128, (j + 1) * 128)
        for g in range(requests // BLOCK):
            put, at = [], []
            for r in range(g * BLOCK, (g + 1) * BLOCK):
                put.append(jnp.where(hi_ref[r : r + 1, lanes] == side, val_ref[r : r + 1, lanes], 0.0))
                at.append(jnp.where(lo_ref[r : r + 1, lanes] == side, 1.0, 0.0))
            table += dot_t(
                jnp.concatenate(put, axis=0).astype(bf16), jnp.concatenate(at, axis=0).astype(bf16)
            )
    same = iota((wide, wide), 0) // SIDE == iota((wide, wide), 1) // SIDE
    table = jnp.where(same, table, 0.0).astype(bf16)
    span = SIDE * page
    spread = jnp.where(
        iota((wide, span), 0) % SIDE == iota((wide, span), 1) // page, 1.0, 0.0
    ).astype(bf16)
    found = dot(table, spread)
    code = found[:SIDE]
    for b in range(1, BLOCK):
        code = code + found[b * SIDE : (b + 1) * SIDE]
    code = code.astype(jnp.int32) - 1
    key_ref[...] = jnp.where(iota(code.shape, 1) % page <= (code & (page - 1)), code >> 4, -1)

    turn_row = iota((rows, rows), 0)
    turn = jnp.where(
        iota((rows, rows), 1) == (turn_row % requests) * heads + turn_row // requests, 1.0, 0.0
    )
    q = dot(turn.astype(bf16), q_ref[...]).astype(bf16)
    scale = math.log2(math.e) / math.sqrt(dim)
    per = CHUNK // span
    wanted = iota((requests, span), 0)

    def scores(c):
        parts = []
        for i in range(per):
            s = dot_t(q, k_buf[c * CHUNK + i * span : c * CHUNK + (i + 1) * span, :])
            key = key_ref[c * per + i : c * per + i + 1, :]
            bias = jnp.where(key == wanted, 0.0, masked)
            parts.append(s + jnp.concatenate([bias] * heads, axis=0))
        return parts

    top = jnp.full((rows, 1), lowest, f32)
    total = jnp.zeros((rows, 1), f32)
    out = jnp.zeros((rows, dim), f32)
    copies[0][0].wait()
    now = scores(0)
    for c in range(steps):
        if c + 1 < steps:
            copies[c + 1][0].wait()
        copies[c][1].wait()
        after = scores(c + 1) if c + 1 < steps else None
        highest = now[0]
        for s in now[1:]:
            highest = jnp.maximum(highest, s)
        new_top = jnp.maximum(top, jnp.max(highest, axis=1, keepdims=True))
        keep = jnp.exp2((top - new_top) * scale)
        out = out * keep
        summed = None
        for i, s in enumerate(now):
            p = jnp.exp2((s - new_top) * scale)
            summed = p if summed is None else summed + p
            v = v_buf[c * CHUNK + i * span : c * CHUNK + (i + 1) * span, :]
            out = out + dot(p.astype(bf16), v)
        total = total * keep + jnp.sum(summed, axis=1, keepdims=True)
        top = new_top
        now = after

    nk = jnp.concatenate([nk_ref[...].astype(f32)] * heads, axis=0)
    nv = jnp.concatenate([nv_ref[...].astype(f32)] * heads, axis=0)
    self_score = jnp.sum(q.astype(f32) * nk, axis=1, keepdims=True)
    self_score = jnp.where(me == 0, self_score, masked)
    new_top = jnp.maximum(top, self_score)
    keep = jnp.exp2((top - new_top) * scale)
    take = jnp.exp2((self_score - new_top) * scale)
    out = out * keep + take * nv
    total = total * keep + take

    lane = iota((rows, 128), 1)
    group = (iota((rows, 128), 0) // requests) % 3
    meta = jnp.zeros((rows, 128), f32)
    for i, part in enumerate(split3(new_top) + split3(total)):
        meta = jnp.where(lane == 6 * group + i, part, meta)
    both = jnp.concatenate([out.astype(bf16), meta.astype(bf16)], axis=0)
    sent = out_ref.shape[0]
    to = iota((sent, 2 * rows), 0)
    source = iota((sent, 2 * rows), 1)
    inner = jnp.where(source < rows, source, source - rows)
    flat = (inner % requests) * heads + inner // requests
    data = (source < rows) & (to % 4 < 3) & (flat == (to // 4) * 3 + to % 4)
    head_row = (source >= rows) & (to % 4 == 3) & (flat // 3 == to // 4)
    pick = jnp.where(data, 1.0, jnp.where(head_row, 1.0, 0.0)).astype(bf16)
    out_ref[...] = dot(pick, both).astype(bf16)


def near_kernel(got_ref, out_ref, *, scale):
    sent = got_ref.shape[0]
    blocks = sent // (4 * NEAR)
    mine = 3 * blocks
    kept = out_ref.shape[1]
    got = got_ref[...]
    height = 2 * NEAR * kept
    to = iota((height, sent), 0)
    source = iota((height, sent), 1)
    line = to % kept
    near = (to // kept) % NEAR
    base = (line // 3) * (4 * NEAR) + near * 4
    wanted = jnp.where(to < NEAR * kept, base + line % 3, base + 3)
    pick = jnp.where((source == wanted) & (line < mine), 1.0, 0.0).astype(bf16)
    all_rows = dot(pick, got)
    lane = iota((kept, 128), 1)
    line = iota((kept, 128), 0)
    first = 6 * (line % 3)
    outs, tops, totals = [], [], []
    for b in range(NEAR):
        outs.append(all_rows[b * kept : (b + 1) * kept])
        meta = all_rows[(NEAR + b) * kept : (NEAR + b + 1) * kept]
        is_top = (lane >= first) & (lane < first + 3)
        is_total = (lane >= first + 3) & (lane < first + 6)
        tops.append(jnp.sum(jnp.where(is_top, meta, 0.0), axis=1, keepdims=True))
        totals.append(jnp.sum(jnp.where(is_total, meta, 0.0), axis=1, keepdims=True))
    top = tops[0]
    for t in tops[1:]:
        top = jnp.maximum(top, t)
    out = jnp.zeros((kept, 128), f32)
    total = jnp.zeros((kept, 1), f32)
    for b in range(NEAR):
        factor = jnp.exp2((tops[b] - top) * scale)
        out = out + factor * outs[b]
        total = total + factor * totals[b]
    for i, part in enumerate(split3(top) + split3(total)):
        across = jnp.sum(jnp.where(lane == line, part, 0.0), axis=0, keepdims=True)
        out = jnp.where(line == mine + i, across, out)
    out = out.astype(bf16)
    for d in range(out_ref.shape[0]):
        out_ref[d] = out


def project_kernel(got_ref, w_hbm, out_ref, w_buf, flat_ref, sems, *, scale):
    peers, kept, dim = got_ref.shape
    far = peers // NEAR
    mine = kept - 8
    inner = w_hbm.shape[0]
    piece = inner // W_CHUNKS
    copies = []
    for c in range(W_CHUNKS):
        part = pl.ds(c * piece, piece)
        copy = pltpu.make_async_copy(w_hbm.at[part], w_buf.at[part], sems.at[c])
        copy.start()
        copies.append(copy)
    flat_ref[...] = jnp.zeros(flat_ref.shape, f32)
    lane = iota((kept, 128), 1)
    line = iota((kept, 128), 0)
    for b in range(NEAR):
        outs, tops, totals = [], [], []
        for a in range(far):
            x = got_ref[a * NEAR + b].astype(f32)
            head = x[mine : mine + 8]
            top = head[0:1] + head[1:2] + head[2:3]
            total = head[3:4] + head[4:5] + head[5:6]
            outs.append(x)
            tops.append(jnp.sum(jnp.where(lane == line, top, 0.0), axis=1, keepdims=True))
            totals.append(jnp.sum(jnp.where(lane == line, total, 0.0), axis=1, keepdims=True))
        top = tops[0]
        for t in tops[1:]:
            top = jnp.maximum(top, t)
        out = jnp.zeros((kept, dim), f32)
        total = jnp.zeros((kept, 1), f32)
        for a in range(far):
            factor = jnp.exp2((tops[a] - top) * scale)
            out = out + factor * outs[a]
            total = total + factor * totals[a]
        attended = out / total
        halves = NEAR // 2
        request, half = b // halves, b % halves
        for i in range(mine):
            at = ((i // 3) * 3 * halves + half * 3 + i % 3) * dim
            flat_ref[request : request + 1, at : at + dim] = attended[i : i + 1]
    acc = jnp.zeros((8, w_hbm.shape[1]), f32)
    for c in range(W_CHUNKS):
        copies[c].wait()
        lhs = flat_ref[:, c * piece : (c + 1) * piece].astype(bf16)
        acc = acc + dot(lhs, w_buf[c * piece : (c + 1) * piece, :])
    out_ref[...] = acc[: out_ref.shape[0]].astype(bf16)


VMEM = pl.BlockSpec(memory_space=pltpu.VMEM)
SMEM = pl.BlockSpec(memory_space=pltpu.SMEM)
ANY = pl.BlockSpec(memory_space=pl.ANY)


def local(
    queries, k_cache, v_cache, new_key, new_value, ctx_lens, page_owner, page_slot, out_weight,
    interpret=False,
):
    _, slots, page, dim = k_cache.shape
    requests, heads, _ = queries.shape
    tokens = slots * page
    rows = requests * heads
    me = lax.axis_index(("far", "near")).astype(jnp.int32).reshape(1)
    sent = rows // 3 * 4
    scale = math.log2(math.e) / math.sqrt(dim)
    partial = attend_call(
        me, ctx_lens, page_owner, page_slot, queries.reshape(rows, dim), new_key[0], new_value[0],
        k_cache.reshape(tokens, dim), v_cache.reshape(tokens, dim), sent, interpret,
    )
    got = lax.all_to_all(partial, ("heads", "near"), 0, 0, tiled=True)
    peers = lax.axis_size("far") * lax.axis_size("near")
    merged = near_call(got, peers, scale, interpret)
    everything = lax.all_to_all(merged, ("far", "near"), 0, 0, tiled=True)
    mine = requests // lax.axis_size("heads")
    return project_call(everything, out_weight, mine, scale, interpret)


def attend_call(me, lens, owner, slot, q, nk, nv, k, v, sent, interpret):
    tokens, dim = k.shape
    requests, max_pages = owner.shape
    return pl.pallas_call(
        attend_kernel,
        out_shape=jax.ShapeDtypeStruct((sent, dim), bf16),
        in_specs=[SMEM, SMEM, VMEM, VMEM, VMEM, VMEM, VMEM, ANY, ANY],
        out_specs=VMEM,
        scratch_shapes=[
            pltpu.VMEM((tokens, dim), bf16),
            pltpu.VMEM((tokens, dim), bf16),
            pltpu.VMEM((requests, max_pages), jnp.int32),
            pltpu.VMEM((requests, max_pages), jnp.int32),
            pltpu.VMEM((requests, max_pages), f32),
            pltpu.VMEM((SIDE, tokens // SIDE), jnp.int32),
            pltpu.SemaphoreType.DMA((2, tokens // CHUNK)),
        ],
        interpret=interpret,
        name="attend",
    )(me, lens, owner, slot, q, nk, nv, k, v)


def near_call(got, peers, scale, interpret):
    sent, dim = got.shape
    kept = sent // (4 * NEAR) * 3 + 8
    return pl.pallas_call(
        lambda *refs: near_kernel(*refs, scale=scale),
        out_shape=jax.ShapeDtypeStruct((peers, kept, dim), bf16),
        in_specs=[VMEM],
        out_specs=VMEM,
        interpret=interpret,
        name="near",
    )(got)


def project_call(everything, w, mine, scale, interpret):
    inner, features = w.shape
    return pl.pallas_call(
        lambda *refs: project_kernel(*refs, scale=scale),
        out_shape=jax.ShapeDtypeStruct((mine, features), bf16),
        in_specs=[VMEM, ANY],
        out_specs=VMEM,
        scratch_shapes=[
            pltpu.VMEM((inner, features), bf16),
            pltpu.VMEM((8, inner), f32),
            pltpu.SemaphoreType.DMA((W_CHUNKS,)),
        ],
        interpret=interpret,
        name="project",
    )(everything, w)


def solution(mesh):
    torus = Mesh(
        mesh.devices.reshape(
            mesh.shape["group"], mesh.shape["pages"] // NEAR, NEAR, mesh.shape["heads"]
        ),
        ("group", "far", "near", "heads"),
    )
    pages = ("far", "near")
    in_specs = (
        P("group", "heads", None),
        P("heads", ("group", *pages), None, None),
        P("heads", ("group", *pages), None, None),
        P("heads", "group", None),
        P("heads", "group", None),
        P("group"),
        P("group", None),
        P("group", None),
        P(None, pages),
    )
    out_specs = P(("group", "heads"), pages)
    return jax.shard_map(local, mesh=torus, in_specs=in_specs, out_specs=out_specs, check_vma=False)
```

time: 172 us -> 69.6 us (0.40)
  other arithmetic: 52.4 us -> 0 us
  local copies, waits for them, and re-layouts: 25.4 us -> 1.36 us
  matrix products: 20.4 us -> 0 us
  Pallas kernels: 0 us -> 13.5 us
  blocking collectives: 66.7 us -> 54.3 us
  loops' own time: 6.63 us -> 0 us
    all_gather x1 -> x0, blocking collectives: 53.1 us -> none  [gathered_once(): both, at, found = (lax.all_gather(jnp.concatenate(lines), axis), 0, {})]
    all_to_all x2, blocking collectives: 13.5 us -> 54.3 us  [the longest x1 34.7 us: local(): everything = lax.all_to_all(merged, ('far', 'near'), 0, 0, tiled=True)]
    reduce_max x10 -> x0, other arithmetic: 33.3 us -> none  [the longest x8 33 us: one_block(): length = jnp.max(jnp.where(matched, entry_length[None, :], 0), axis=1)]
    dot_general x7 -> x0, matrix products: 20.4 us -> none  [the longest x1 6.59 us: local(): jnp.einsum('pkgt,kptd->pkgd', weights.astype(jnp.bfloat16), v_cache, pref...]
    reduce_sum x1 -> x0, other arithmetic: 15.7 us -> none  [local(): page_total = jnp.sum(weights, axis=3)]
    pallas_call x0 -> x3, Pallas kernels: none -> 13.5 us  [the longest x1 7.66 us: attend_call(): pl.pallas_call(attend_kernel, out_shape=jax.ShapeDtypeStruct((sent, dim),...]
    while x60 -> x0, local copies, waits for them, and re-layouts: 6.91 us -> none
    another operation x2 -> x0, loops' own time: 6.63 us -> none  [the longest x1 6.09 us: slot_tables(): lax.map(one_block, jnp.arange(block_count, dtype=jnp.int32))]
where the time goes in v1:
time: 69.6 us; the launch traced here: 69.2 us
  blocking collectives  54.3 us (78%)
  Pallas kernels  13.5 us (19%)
  local copies, waits for them, and re-layouts  1.36 us (2%)
    all_to_all x1, blocking collectives, local(): everything = lax.all_to_all(merged, ('far', 'near'), 0, 0, tiled=True)  34.7 us
    all_to_all x1, blocking collectives, local(): got = lax.all_to_all(partial, ('heads', 'near'), 0, 0, tiled=True)  19.6 us
    pallas_call x1, Pallas kernels, attend_call(): pl.pallas_call(attend_kernel, out_shape=jax.ShapeDtypeStruct((sent, dim),...  7.66 us
    pallas_call x1, Pallas kernels, project_call(): pl.pallas_call(lambda *refs: project_kernel(*refs, scale=scale), out_shap...  4.15 us
    pallas_call x1, Pallas kernels, near_call(): pl.pallas_call(lambda *refs: near_kernel(*refs, scale=scale), out_shape=j...  1.67 us

profile of v1, /device:TPU:40, one launch (start us, length us, event | category | flops | bytes accessed | tf_op | source)
XLA Modules:
  0.0 69.2 jit_solution(4416319853814205412)
XLA Ops:
  0.0 0.7 %copy.11 = bf16[16,6,128]{2,1,0:T(8,128)(2,1)S(1)} copy(bf16[16,6,128]{2,0,1:T(8,128)(2,1)} %param.9) | data formatting | bytes 49152 | tf_op args[0]
  0.7 0.6 reshape.15.q_ref
  1.4 7.7 %attend.1 = bf16[128,128]{1,0:T(8,128)(2,1)} custom-call(s32[1]{0:T(128)} %bitcast.me_ref, s32[16]{0:T(128)} %lens_ref.1, s32[16,1024]{1,0:T(8,128)} %owner_ref.1, s32[16,1024]{1,0:T(8,128)} %slot_ref.1, bf16[96,128]{1,0:T(8,128)(2,1)} %reshape.15.q_ref, bf16[16,128]{1,0:T(8,128)(2,1)} %bitcast.11, bf16[16,128]{1,0:T(8,128)(2,1)} %bitcast.12, ...), custom_call_target="tpu_custom_call" | custom-call | tf_op jit(solution)/shard_map/attend/pallas_call | solution.py:293
  9.0 19.6 %all_to_all.16 = bf16[32,4,128]{2,1,0:T(4,128)(2,1)} all-to-all(bf16[32,4,128]{2,1,0:T(4,128)(2,1)} %bitcast.9), channel_id=1, replica_groups=mesh['group'=2,'far'=4,'near'=4,'heads'=8] {'heads','near'}, dimensions={0} | all-to-all | bytes 65536 | tf_op jit(solution)/shard_map/all_to_all | solution.py:282
  28.6 1.7 %near.1 = bf16[16,32,128]{2,1,0:T(8,128)(2,1)} custom-call(bf16[128,128]{1,0:T(8,128)(2,1)} %bitcast.10), custom_call_target="tpu_custom_call" | custom-call | tf_op jit(solution)/shard_map/near/pallas_call | solution.py:315
  30.3 34.7 %all_to_all.17.refs_0_ = bf16[16,32,128]{2,1,0:T(8,128)(2,1)} all-to-all(bf16[16,32,128]{2,1,0:T(8,128)(2,1)} %near.1), channel_id=1, replica_groups=mesh['group'=2,'far'=4,'near'=4,'heads'=8] {'far','near'}, dimensions={0} | all-to-all | bytes 262144 | tf_op jit(solution)/shard_map/all_to_all | solution.py:285
  65.0 4.2 %project.1 = bf16[2,384]{1,0:T(2,128)(2,1)} custom-call(bf16[16,32,128]{2,1,0:T(8,128)(2,1)} %all_to_all.17.refs_0_, bf16[6144,384]{1,0:T(8,128)(2,1)} %refs_1_.1), custom_call_target="tpu_custom_call" | custom-call | tf_op jit(solution)/shard_map/project/pallas_call | solution.py:327

commit v2 on v1

--- a/solution.py
+++ b/solution.py
@@ -9,10 +9,9 @@
 from jax.sharding import PartitionSpec as P
 
 NEAR = 4
-CHUNK = 2048
+CHUNK = 4096
 SIDE = 32
 BLOCK = 8
-W_CHUNKS = 6
 
 f32 = jnp.float32
 bf16 = jnp.bfloat16
@@ -40,8 +39,9 @@
 
 
 def attend_kernel(
-    me_ref, lens_ref, owner_ref, slot_ref, q_ref, nk_ref, nv_ref, k_hbm, v_hbm, out_ref,
-    k_buf, v_buf, hi_ref, lo_ref, val_ref, key_ref, sems,
+    lens_hbm, owner_hbm, slot_hbm, q_hbm, nk_hbm, nv_hbm, k_hbm, v_hbm, out_ref,
+    lens_ref, owner_ref, slot_ref, q_ref, nk_ref, nv_ref,
+    k_buf, v_buf, hi_ref, lo_ref, val_ref, key_ref, small_sems, sems, *, position,
 ):
     requests, max_pages = owner_ref.shape
     rows, dim = q_ref.shape
@@ -50,6 +50,19 @@
     page = tokens // (SIDE * SIDE)
     steps = tokens // CHUNK
     copies = []
+    small = [
+        pltpu.make_async_copy(source, target, small_sems.at[i])
+        for i, (source, target) in enumerate(
+            [
+                (lens_hbm, lens_ref), (owner_hbm, owner_ref), (slot_hbm, slot_ref),
+                (q_hbm, q_ref), (nk_hbm, nk_ref), (nv_hbm, nv_ref),
+            ]
+        )
+    ]
+    for copy in small:
+        copy.start()
+    for copy in small:
+        copy.wait()
     for c in range(steps):
         part = pl.ds(c * CHUNK, CHUNK)
         pair = (
@@ -60,7 +73,7 @@
             copy.start()
         copies.append(pair)
 
-    me = me_ref[0]
+    me = position()
     row = iota((requests, 128), 0)
     lens = jnp.zeros((requests, 128), jnp.int32)
     for r in range(requests):
@@ -97,11 +110,7 @@
     code = code.astype(jnp.int32) - 1
     key_ref[...] = jnp.where(iota(code.shape, 1) % page <= (code & (page - 1)), code >> 4, -1)
 
-    turn_row = iota((rows, rows), 0)
-    turn = jnp.where(
-        iota((rows, rows), 1) == (turn_row % requests) * heads + turn_row // requests, 1.0, 0.0
-    )
-    q = dot(turn.astype(bf16), q_ref[...]).astype(bf16)
+    q = q_ref[...]
     scale = math.log2(math.e) / math.sqrt(dim)
     per = CHUNK // span
     wanted = iota((requests, span), 0)
@@ -211,18 +220,10 @@
         out_ref[d] = out
 
 
-def project_kernel(got_ref, w_hbm, out_ref, w_buf, flat_ref, sems, *, scale):
+def project_kernel(got_ref, w_ref, out_ref, flat_ref, *, scale):
     peers, kept, dim = got_ref.shape
     far = peers // NEAR
     mine = kept - 8
-    inner = w_hbm.shape[0]
-    piece = inner // W_CHUNKS
-    copies = []
-    for c in range(W_CHUNKS):
-        part = pl.ds(c * piece, piece)
-        copy = pltpu.make_async_copy(w_hbm.at[part], w_buf.at[part], sems.at[c])
-        copy.start()
-        copies.append(copy)
     flat_ref[...] = jnp.zeros(flat_ref.shape, f32)
     lane = iota((kept, 128), 1)
     line = iota((kept, 128), 0)
@@ -251,16 +252,11 @@
         for i in range(mine):
             at = ((i // 3) * 3 * halves + half * 3 + i % 3) * dim
             flat_ref[request : request + 1, at : at + dim] = attended[i : i + 1]
-    acc = jnp.zeros((8, w_hbm.shape[1]), f32)
-    for c in range(W_CHUNKS):
-        copies[c].wait()
-        lhs = flat_ref[:, c * piece : (c + 1) * piece].astype(bf16)
-        acc = acc + dot(lhs, w_buf[c * piece : (c + 1) * piece, :])
-    out_ref[...] = acc[: out_ref.shape[0]].astype(bf16)
+    projected = dot(flat_ref[...].astype(bf16), w_ref[...])
+    out_ref[...] = projected[: out_ref.shape[0]].astype(bf16)
 
 
 VMEM = pl.BlockSpec(memory_space=pltpu.VMEM)
-SMEM = pl.BlockSpec(memory_space=pltpu.SMEM)
 ANY = pl.BlockSpec(memory_space=pl.ANY)
 
 
@@ -272,13 +268,13 @@
     requests, heads, _ = queries.shape
     tokens = slots * page
     rows = requests * heads
-    me = lax.axis_index(("far", "near")).astype(jnp.int32).reshape(1)
     sent = rows // 3 * 4
     scale = math.log2(math.e) / math.sqrt(dim)
     partial = attend_call(
-        me, ctx_lens, page_owner, page_slot, queries.reshape(rows, dim), new_key[0], new_value[0],
+        lambda: lax.axis_index(("far", "near")), ctx_lens, page_owner, page_slot, queries.transpose(1, 0, 2).reshape(rows, dim), new_key[0], new_value[0],
         k_cache.reshape(tokens, dim), v_cache.reshape(tokens, dim), sent, interpret,
     )
+    partial, out_weight = lax.optimization_barrier((partial, out_weight))
     got = lax.all_to_all(partial, ("heads", "near"), 0, 0, tiled=True)
     peers = lax.axis_size("far") * lax.axis_size("near")
     merged = near_call(got, peers, scale, interpret)
@@ -287,26 +283,34 @@
     return project_call(everything, out_weight, mine, scale, interpret)
 
 
-def attend_call(me, lens, owner, slot, q, nk, nv, k, v, sent, interpret):
+def in_hbm(x):
+    return pltpu.with_memory_space_constraint(x, pltpu.HBM)
+
+
+def attend_call(position, lens, owner, slot, q, nk, nv, k, v, sent, interpret):
     tokens, dim = k.shape
     requests, max_pages = owner.shape
     return pl.pallas_call(
-        attend_kernel,
+        lambda *refs: attend_kernel(*refs, position=position),
         out_shape=jax.ShapeDtypeStruct((sent, dim), bf16),
-        in_specs=[SMEM, SMEM, VMEM, VMEM, VMEM, VMEM, VMEM, ANY, ANY],
+        in_specs=[ANY] * 8,
         out_specs=VMEM,
         scratch_shapes=[
+            pltpu.SMEM(lens.shape, lens.dtype),
+            *(pltpu.VMEM(x.shape, x.dtype) for x in (owner, slot, q, nk, nv)),
             pltpu.VMEM((tokens, dim), bf16),
             pltpu.VMEM((tokens, dim), bf16),
             pltpu.VMEM((requests, max_pages), jnp.int32),
             pltpu.VMEM((requests, max_pages), jnp.int32),
             pltpu.VMEM((requests, max_pages), f32),
             pltpu.VMEM((SIDE, tokens // SIDE), jnp.int32),
+            pltpu.SemaphoreType.DMA((6,)),
             pltpu.SemaphoreType.DMA((2, tokens // CHUNK)),
         ],
+        compiler_params=pltpu.CompilerParams(vmem_limit_bytes=24 << 20),
         interpret=interpret,
         name="attend",
-    )(me, lens, owner, slot, q, nk, nv, k, v)
+    )(*(in_hbm(x) for x in (lens, owner, slot, q, nk, nv, k, v)))
 
 
 def near_call(got, peers, scale, interpret):
@@ -317,6 +321,7 @@
         out_shape=jax.ShapeDtypeStruct((peers, kept, dim), bf16),
         in_specs=[VMEM],
         out_specs=VMEM,
+        compiler_params=pltpu.CompilerParams(vmem_limit_bytes=4 << 20),
         interpret=interpret,
         name="near",
     )(got)
@@ -327,16 +332,13 @@
     return pl.pallas_call(
         lambda *refs: project_kernel(*refs, scale=scale),
         out_shape=jax.ShapeDtypeStruct((mine, features), bf16),
-        in_specs=[VMEM, ANY],
+        in_specs=[VMEM, VMEM],
         out_specs=VMEM,
-        scratch_shapes=[
-            pltpu.VMEM((inner, features), bf16),
-            pltpu.VMEM((8, inner), f32),
-            pltpu.SemaphoreType.DMA((W_CHUNKS,)),
-        ],
+        scratch_shapes=[pltpu.VMEM((8, inner), f32)],
+        compiler_params=pltpu.CompilerParams(vmem_limit_bytes=8 << 20),
         interpret=interpret,
         name="project",
-    )(everything, w)
+    )(everything, pltpu.with_memory_space_constraint(w, pltpu.VMEM))
 
 
 def solution(mesh):

time: 69.6 us -> 62.3 us (0.90)
  Pallas kernels: 13.5 us -> 8.44 us
  local copies, waits for them, and re-layouts: 1.36 us -> 0.01 us
    pallas_call x1, Pallas kernels: 4.15 us -> 1.38 us  [project_call(): pl.pallas_call(lambda *refs: project_kernel(*refs, scale=scale), out_shap...]
    pallas_call x1, Pallas kernels: 1.67 us -> 0.27 us  [near_call(): pl.pallas_call(lambda *refs: near_kernel(*refs, scale=scale), out_shape=j...]
    pallas_call x1, Pallas kernels: 7.66 us -> 6.79 us  [attend_call(): pl.pallas_call(lambda *refs: attend_kernel(*refs, position=position), out...]
    unnamed x1 -> x2, local copies, waits for them, and re-layouts: 0.75 us -> 0.01 us
where the time goes in v2:
time: 62.3 us; the launch traced here: 62.2 us
  blocking collectives  53.7 us (86%)
  Pallas kernels  8.44 us (14%)
    all_to_all x1, blocking collectives, local(): everything = lax.all_to_all(merged, ('far', 'near'), 0, 0, tiled=True)  34.4 us
    all_to_all x1, blocking collectives, local(): got = lax.all_to_all(partial, ('heads', 'near'), 0, 0, tiled=True)  19.3 us
    pallas_call x1, Pallas kernels, attend_call(): pl.pallas_call(lambda *refs: attend_kernel(*refs, position=position), out...  6.79 us
    pallas_call x1, Pallas kernels, project_call(): pl.pallas_call(lambda *refs: project_kernel(*refs, scale=scale), out_shap...  1.38 us

profile of v2, /device:TPU:40, one launch (start us, length us, event | category | flops | bytes accessed | tf_op | source)
XLA Modules:
  0.0 62.2 jit_solution(6375526268378518272)
XLA Ops:
  0.0 0.0 copy-start
  0.0 6.8 %attend.1 = bf16[128,128]{1,0:T(8,128)(2,1)S(1)} custom-call(s32[16]{0:T(128)} %refs_0_.1, s32[16,1024]{1,0:T(8,128)} %refs_1_.1, s32[16,1024]{1,0:T(8,128)} %refs_2_.1, bf16[96,128]{1,0:T(8,128)(2,1)} %bitcast.13, bf16[16,128]{1,0:T(8,128)(2,1)} %bitcast.14, bf16[16,128]{1,0:T(8,128)(2,1)} %bitcast.15, bf16[16384,128]{1,0:T(8,128)(2,1)} %bitcast.11, ...), custom_call_target="tpu_custom_call" | custom-call | tf_op jit(solution)/shard_map/attend/pallas_call | solution.py:293
  6.8 19.3 %all_to_all.16 = bf16[32,4,128]{2,1,0:T(4,128)(2,1)S(1)} all-to-all(bf16[32,4,128]{2,1,0:T(4,128)(2,1)S(1)} %bitcast.9), channel_id=1, replica_groups=mesh['group'=2,'far'=4,'near'=4,'heads'=8] {'heads','near'}, dimensions={0} | all-to-all | bytes 65536 | tf_op jit(solution)/shard_map/all_to_all | solution.py:278
  26.1 0.3 near.1
  26.4 34.4 %all_to_all.17.refs_0_ = bf16[16,32,128]{2,1,0:T(8,128)(2,1)S(1)} all-to-all(bf16[16,32,128]{2,1,0:T(8,128)(2,1)S(1)} %near.1), channel_id=1, replica_groups=mesh['group'=2,'far'=4,'near'=4,'heads'=8] {'far','near'}, dimensions={0} | all-to-all | bytes 262144 | tf_op jit(solution)/shard_map/all_to_all | solution.py:281
  60.8 0.0 copy-done
  60.8 1.4 %project.1 = bf16[2,384]{1,0:T(2,128)(2,1)} custom-call(bf16[16,32,128]{2,1,0:T(8,128)(2,1)S(1)} %all_to_all.17.refs_0_, bf16[6144,384]{1,0:T(8,128)(2,1)S(1)} %copy-done), custom_call_target="tpu_custom_call" | custom-call | tf_op jit(solution)/shard_map/project/pallas_call | solution.py:332
Async XLA Ops:
  0.0 60.8 %copy-start = (bf16[6144,384]{1,0:T(8,128)(2,1)S(1)}, bf16[6144,384]{1,0:T(8,128)(2,1)}, u32[]{:S(2)}) copy-start(bf16[6144,384]{1,0:T(8,128)(2,1)} %refs_1_.2) | copy-start | bytes 14155780

commit v3 on v2

--- a/solution.py
+++ b/solution.py
@@ -11,7 +11,8 @@
 NEAR = 4
 CHUNK = 4096
 SIDE = 32
-BLOCK = 8
+BLOCK = 4
+ENTRIES = 256
 
 f32 = jnp.float32
 bf16 = jnp.bfloat16
@@ -84,11 +85,11 @@
     hi_ref[...] = slot_ref[...] >> 5
     lo_ref[...] = slot_ref[...] & 31
     val_ref[...] = val.astype(f32)
-    side = iota((SIDE, 128), 0)
+    side = iota((SIDE, ENTRIES), 0)
     wide = BLOCK * SIDE
     table = jnp.zeros((wide, wide), f32)
-    for j in range(max_pages // 128):
-        lanes = slice(j * 128, (j + 1) * 128)
+    for j in range(max_pages // ENTRIES):
+        lanes = slice(j * ENTRIES, (j + 1) * ENTRIES)
         for g in range(requests // BLOCK):
             put, at = [], []
             for r in range(g * BLOCK, (g + 1) * BLOCK):
@@ -181,7 +182,7 @@
     sent = got_ref.shape[0]
     blocks = sent // (4 * NEAR)
     mine = 3 * blocks
-    kept = out_ref.shape[1]
+    kept = mine + 8
     got = got_ref[...]
     height = 2 * NEAR * kept
     to = iota((height, sent), 0)
@@ -212,36 +213,39 @@
         factor = jnp.exp2((tops[b] - top) * scale)
         out = out + factor * outs[b]
         total = total + factor * totals[b]
-    for i, part in enumerate(split3(top) + split3(total)):
-        across = jnp.sum(jnp.where(lane == line, part, 0.0), axis=0, keepdims=True)
-        out = jnp.where(line == mine + i, across, out)
-    out = out.astype(bf16)
-    for d in range(out_ref.shape[0]):
-        out_ref[d] = out
-
-
-def project_kernel(got_ref, w_ref, out_ref, flat_ref, *, scale):
-    peers, kept, dim = got_ref.shape
-    far = peers // NEAR
-    mine = kept - 8
+    meta = jnp.zeros((kept, 128), f32)
+    for i, part in enumerate(split3(top) + split3(total)[:2]):
+        meta = jnp.where((lane == line + i * mine) & (line < mine), part, meta)
+    out = jnp.where(line == mine, jnp.sum(meta, axis=0, keepdims=True), out)
+    block = mine + 2
+    out = out.astype(bf16)[:block]
+    for d in range(out_ref.shape[0] // block):
+        out_ref[d * block : (d + 1) * block, :] = out
+
+
+def project_kernel(got_ref, w_ref, out_ref, flat_ref, *, scale, block):
+    total_rows, dim = got_ref.shape
+    far = total_rows // block // NEAR
+    mine = block - 2
     flat_ref[...] = jnp.zeros(flat_ref.shape, f32)
-    lane = iota((kept, 128), 1)
-    line = iota((kept, 128), 0)
+    lane = iota((mine, 128), 1)
+    line = iota((mine, 128), 0)
+    is_top = (lane % mine == line) & (lane < 3 * mine)
+    is_total = (lane % mine == line) & (lane >= 3 * mine) & (lane < 5 * mine)
     for b in range(NEAR):
         outs, tops, totals = [], [], []
         for a in range(far):
-            x = got_ref[a * NEAR + b].astype(f32)
-            head = x[mine : mine + 8]
-            top = head[0:1] + head[1:2] + head[2:3]
-            total = head[3:4] + head[4:5] + head[5:6]
-            outs.append(x)
-            tops.append(jnp.sum(jnp.where(lane == line, top, 0.0), axis=1, keepdims=True))
-            totals.append(jnp.sum(jnp.where(lane == line, total, 0.0), axis=1, keepdims=True))
+            first = (a * NEAR + b) * block
+            x = got_ref[first : first + block, :].astype(f32)
+            head = x[mine : mine + 1]
+            outs.append(x[:mine])
+            tops.append(jnp.sum(jnp.where(is_top, head, 0.0), axis=1, keepdims=True))
+            totals.append(jnp.sum(jnp.where(is_total, head, 0.0), axis=1, keepdims=True))
         top = tops[0]
         for t in tops[1:]:
             top = jnp.maximum(top, t)
-        out = jnp.zeros((kept, dim), f32)
-        total = jnp.zeros((kept, 1), f32)
+        out = jnp.zeros((mine, dim), f32)
+        total = jnp.zeros((mine, 1), f32)
         for a in range(far):
             factor = jnp.exp2((tops[a] - top) * scale)
             out = out + factor * outs[a]
@@ -278,9 +282,12 @@
     got = lax.all_to_all(partial, ("heads", "near"), 0, 0, tiled=True)
     peers = lax.axis_size("far") * lax.axis_size("near")
     merged = near_call(got, peers, scale, interpret)
+    block = merged.shape[0] // peers
+    merged = merged.reshape(peers, block // 2, 2, dim)
     everything = lax.all_to_all(merged, ("far", "near"), 0, 0, tiled=True)
+    everything = everything.reshape(peers * block, dim)
     mine = requests // lax.axis_size("heads")
-    return project_call(everything, out_weight, mine, scale, interpret)
+    return project_call(everything, out_weight, mine, block, scale, interpret)
 
 
 def in_hbm(x):
@@ -315,10 +322,10 @@
 
 def near_call(got, peers, scale, interpret):
     sent, dim = got.shape
-    kept = sent // (4 * NEAR) * 3 + 8
+    block = sent // (4 * NEAR) * 3 + 2
     return pl.pallas_call(
         lambda *refs: near_kernel(*refs, scale=scale),
-        out_shape=jax.ShapeDtypeStruct((peers, kept, dim), bf16),
+        out_shape=jax.ShapeDtypeStruct((peers * block, dim), bf16),
         in_specs=[VMEM],
         out_specs=VMEM,
         compiler_params=pltpu.CompilerParams(vmem_limit_bytes=4 << 20),
@@ -327,10 +334,10 @@
     )(got)
 
 
-def project_call(everything, w, mine, scale, interpret):
+def project_call(everything, w, mine, block, scale, interpret):
     inner, features = w.shape
     return pl.pallas_call(
-        lambda *refs: project_kernel(*refs, scale=scale),
+        lambda *refs: project_kernel(*refs, scale=scale, block=block),
         out_shape=jax.ShapeDtypeStruct((mine, features), bf16),
         in_specs=[VMEM, VMEM],
         out_specs=VMEM,

time: 62.3 us -> 61.3 us (0.984)
  blocking collectives: 53.7 us -> 52.8 us
    all_to_all x1, blocking collectives: 34.4 us -> 33.5 us  [local(): everything = lax.all_to_all(merged, ('far', 'near'), 0, 0, tiled=True)]
where the time goes in v3:
time: 61.3 us; the launch traced here: 61.2 us
  blocking collectives  52.8 us (86%)
  Pallas kernels  8.34 us (14%)
    all_to_all x1, blocking collectives, local(): everything = lax.all_to_all(merged, ('far', 'near'), 0, 0, tiled=True)  33.5 us
    all_to_all x1, blocking collectives, local(): got = lax.all_to_all(partial, ('heads', 'near'), 0, 0, tiled=True)  19.3 us
    pallas_call x1, Pallas kernels, attend_call(): pl.pallas_call(lambda *refs: attend_kernel(*refs, position=position), out...  6.68 us
    pallas_call x1, Pallas kernels, project_call(): pl.pallas_call(lambda *refs: project_kernel(*refs, scale=scale, block=blo...  1.38 us

profile of v3, /device:TPU:40, one launch (start us, length us, event | category | flops | bytes accessed | tf_op | source)
XLA Modules:
  0.0 61.2 jit_solution(15728440984523573341)
XLA Ops:
  0.0 0.0 copy-start
  0.0 6.7 %attend.1 = bf16[128,128]{1,0:T(8,128)(2,1)S(1)} custom-call(s32[16]{0:T(128)} %refs_0_.1, s32[16,1024]{1,0:T(8,128)} %refs_1_.1, s32[16,1024]{1,0:T(8,128)} %refs_2_.1, bf16[96,128]{1,0:T(8,128)(2,1)} %bitcast.17, bf16[16,128]{1,0:T(8,128)(2,1)} %bitcast.18, bf16[16,128]{1,0:T(8,128)(2,1)} %bitcast.19, bf16[16384,128]{1,0:T(8,128)(2,1)} %bitcast.15, ...), custom_call_target="tpu_custom_call" | custom-call | tf_op jit(solution)/shard_map/attend/pallas_call | solution.py:300
  6.7 19.3 %all_to_all.16 = bf16[32,4,128]{2,1,0:T(4,128)(2,1)S(1)} all-to-all(bf16[32,4,128]{2,1,0:T(4,128)(2,1)S(1)} %bitcast.13), channel_id=1, replica_groups=mesh['group'=2,'far'=4,'near'=4,'heads'=8] {'heads','near'}, dimensions={0} | all-to-all | bytes 65536 | tf_op jit(solution)/shard_map/all_to_all | solution.py:282
  26.0 0.3 near.1
  26.3 33.5 %all_to_all.17 = bf16[16,13,2,128]{3,2,1,0:T(2,128)(2,1)S(1)} all-to-all(bf16[16,13,2,128]{3,2,1,0:T(2,128)(2,1)S(1)} %bitcast.11), channel_id=1, replica_groups=mesh['group'=2,'far'=4,'near'=4,'heads'=8] {'far','near'}, dimensions={0} | all-to-all | bytes 212992 | tf_op jit(solution)/shard_map/all_to_all | solution.py:287
  59.8 0.0 copy-done
  59.8 1.4 %project.1 = bf16[2,384]{1,0:T(2,128)(2,1)} custom-call(bf16[416,128]{1,0:T(8,128)(2,1)S(1)} %bitcast.12, bf16[6144,384]{1,0:T(8,128)(2,1)S(1)} %copy-done), custom_call_target="tpu_custom_call" | custom-call | tf_op jit(solution)/shard_map/project/pallas_call | solution.py:339
Async XLA Ops:
  0.0 59.8 %copy-start = (bf16[6144,384]{1,0:T(8,128)(2,1)S(1)}, bf16[6144,384]{1,0:T(8,128)(2,1)}, u32[]{:S(2)}) copy-start(bf16[6144,384]{1,0:T(8,128)(2,1)} %refs_1_.2) | copy-start | bytes 14155780

commit v4 on v3

--- a/solution.py
+++ b/solution.py
@@ -9,7 +9,8 @@
 from jax.sharding import PartitionSpec as P
 
 NEAR = 4
-CHUNK = 4096
+CHUNK = 8192
+STRIDE = 1024
 SIDE = 32
 BLOCK = 4
 ENTRIES = 256
@@ -42,7 +43,7 @@
 def attend_kernel(
     lens_hbm, owner_hbm, slot_hbm, q_hbm, nk_hbm, nv_hbm, k_hbm, v_hbm, out_ref,
     lens_ref, owner_ref, slot_ref, q_ref, nk_ref, nv_ref,
-    k_buf, v_buf, hi_ref, lo_ref, val_ref, key_ref, small_sems, sems, *, position,
+    k_buf, v_buf, s_buf, hi_ref, lo_ref, val_ref, key_ref, small_sems, sems, *, position,
 ):
     requests, max_pages = owner_ref.shape
     rows, dim = q_ref.shape
@@ -60,19 +61,20 @@
             ]
         )
     ]
+    for c in range(steps):
+        part = pl.ds(c * CHUNK, CHUNK)
+        copies.append((
+            pltpu.make_async_copy(k_hbm.at[part], k_buf.at[part], sems.at[0, c]),
+            pltpu.make_async_copy(v_hbm.at[part], v_buf.at[part], sems.at[1, c]),
+        ))
+    order = [copies[c][kind] for kind in range(2) for c in range(steps)]
     for copy in small:
         copy.start()
+    order[0].start()
     for copy in small:
         copy.wait()
-    for c in range(steps):
-        part = pl.ds(c * CHUNK, CHUNK)
-        pair = (
-            pltpu.make_async_copy(k_hbm.at[part], k_buf.at[part], sems.at[0, c]),
-            pltpu.make_async_copy(v_hbm.at[part], v_buf.at[part], sems.at[1, c]),
-        )
-        for copy in pair:
-            copy.start()
-        copies.append(pair)
+    for copy in order[1:]:
+        copy.start()
 
     me = position()
     row = iota((requests, 128), 0)
@@ -113,51 +115,37 @@
 
     q = q_ref[...]
     scale = math.log2(math.e) / math.sqrt(dim)
-    per = CHUNK // span
     wanted = iota((requests, span), 0)
-
-    def scores(c):
-        parts = []
-        for i in range(per):
-            s = dot_t(q, k_buf[c * CHUNK + i * span : c * CHUNK + (i + 1) * span, :])
-            key = key_ref[c * per + i : c * per + i + 1, :]
-            bias = jnp.where(key == wanted, 0.0, masked)
-            parts.append(s + jnp.concatenate([bias] * heads, axis=0))
-        return parts
-
-    top = jnp.full((rows, 1), lowest, f32)
-    total = jnp.zeros((rows, 1), f32)
+    highest = jnp.full((rows, 128), lowest, f32)
+    for c in range(steps):
+        copies[c][0].wait()
+        for i in range(c * CHUNK // span, (c + 1) * CHUNK // span):
+            here = slice(i * span, (i + 1) * span)
+            bias = jnp.where(key_ref[i : i + 1, :] == wanted, 0.0, masked)
+            s = dot_t(q, k_buf[here, :]) * scale + jnp.concatenate([bias] * heads, axis=0)
+            s_buf[:, here] = s
+            for j in range(span // 128):
+                highest = jnp.maximum(highest, s[:, j * 128 : (j + 1) * 128])
+    top = jnp.max(highest, axis=1, keepdims=True)
+    total = jnp.zeros((rows, 128), f32)
     out = jnp.zeros((rows, dim), f32)
-    copies[0][0].wait()
-    now = scores(0)
     for c in range(steps):
-        if c + 1 < steps:
-            copies[c + 1][0].wait()
         copies[c][1].wait()
-        after = scores(c + 1) if c + 1 < steps else None
-        highest = now[0]
-        for s in now[1:]:
-            highest = jnp.maximum(highest, s)
-        new_top = jnp.maximum(top, jnp.max(highest, axis=1, keepdims=True))
-        keep = jnp.exp2((top - new_top) * scale)
-        out = out * keep
-        summed = None
-        for i, s in enumerate(now):
-            p = jnp.exp2((s - new_top) * scale)
-            summed = p if summed is None else summed + p
-            v = v_buf[c * CHUNK + i * span : c * CHUNK + (i + 1) * span, :]
-            out = out + dot(p.astype(bf16), v)
-        total = total * keep + jnp.sum(summed, axis=1, keepdims=True)
-        top = new_top
-        now = after
+        for i in range(c * CHUNK // STRIDE, (c + 1) * CHUNK // STRIDE):
+            here = slice(i * STRIDE, (i + 1) * STRIDE)
+            p = jnp.exp2(s_buf[:, here] - top)
+            for j in range(STRIDE // 128):
+                total = total + p[:, j * 128 : (j + 1) * 128]
+            out = out + dot(p.astype(bf16), v_buf[here, :])
+    total = jnp.sum(total, axis=1, keepdims=True)
 
     nk = jnp.concatenate([nk_ref[...].astype(f32)] * heads, axis=0)
     nv = jnp.concatenate([nv_ref[...].astype(f32)] * heads, axis=0)
     self_score = jnp.sum(q.astype(f32) * nk, axis=1, keepdims=True)
-    self_score = jnp.where(me == 0, self_score, masked)
+    self_score = jnp.where(me == 0, self_score * scale, masked)
     new_top = jnp.maximum(top, self_score)
-    keep = jnp.exp2((top - new_top) * scale)
-    take = jnp.exp2((self_score - new_top) * scale)
+    keep = jnp.exp2(top - new_top)
+    take = jnp.exp2(self_score - new_top)
     out = out * keep + take * nv
     total = total * keep + take
 
@@ -178,7 +166,7 @@
     out_ref[...] = dot(pick, both).astype(bf16)
 
 
-def near_kernel(got_ref, out_ref, *, scale):
+def near_kernel(got_ref, out_ref):
     sent = got_ref.shape[0]
     blocks = sent // (4 * NEAR)
     mine = 3 * blocks
@@ -210,7 +198,7 @@
     out = jnp.zeros((kept, 128), f32)
     total = jnp.zeros((kept, 1), f32)
     for b in range(NEAR):
-        factor = jnp.exp2((tops[b] - top) * scale)
+        factor = jnp.exp2(tops[b] - top)
         out = out + factor * outs[b]
         total = total + factor * totals[b]
     meta = jnp.zeros((kept, 128), f32)
@@ -223,7 +211,7 @@
         out_ref[d * block : (d + 1) * block, :] = out
 
 
-def project_kernel(got_ref, w_ref, out_ref, flat_ref, *, scale, block):
+def project_kernel(got_ref, w_ref, out_ref, flat_ref, *, block):
     total_rows, dim = got_ref.shape
     far = total_rows // block // NEAR
     mine = block - 2
@@ -247,7 +235,7 @@
         out = jnp.zeros((mine, dim), f32)
         total = jnp.zeros((mine, 1), f32)
         for a in range(far):
-            factor = jnp.exp2((tops[a] - top) * scale)
+            factor = jnp.exp2(tops[a] - top)
             out = out + factor * outs[a]
             total = total + factor * totals[a]
         attended = out / total
@@ -273,7 +261,6 @@
     tokens = slots * page
     rows = requests * heads
     sent = rows // 3 * 4
-    scale = math.log2(math.e) / math.sqrt(dim)
     partial = attend_call(
         lambda: lax.axis_index(("far", "near")), ctx_lens, page_owner, page_slot, queries.transpose(1, 0, 2).reshape(rows, dim), new_key[0], new_value[0],
         k_cache.reshape(tokens, dim), v_cache.reshape(tokens, dim), sent, interpret,
@@ -281,13 +268,13 @@
     partial, out_weight = lax.optimization_barrier((partial, out_weight))
     got = lax.all_to_all(partial, ("heads", "near"), 0, 0, tiled=True)
     peers = lax.axis_size("far") * lax.axis_size("near")
-    merged = near_call(got, peers, scale, interpret)
+    merged = near_call(got, peers, interpret)
     block = merged.shape[0] // peers
     merged = merged.reshape(peers, block // 2, 2, dim)
     everything = lax.all_to_all(merged, ("far", "near"), 0, 0, tiled=True)
     everything = everything.reshape(peers * block, dim)
     mine = requests // lax.axis_size("heads")
-    return project_call(everything, out_weight, mine, block, scale, interpret)
+    return project_call(everything, out_weight, mine, block, interpret)
 
 
 def in_hbm(x):
@@ -307,6 +294,7 @@
             *(pltpu.VMEM(x.shape, x.dtype) for x in (owner, slot, q, nk, nv)),
             pltpu.VMEM((tokens, dim), bf16),
             pltpu.VMEM((tokens, dim), bf16),
+            pltpu.VMEM((q.shape[0], tokens), f32),
             pltpu.VMEM((requests, max_pages), jnp.int32),
             pltpu.VMEM((requests, max_pages), jnp.int32),
             pltpu.VMEM((requests, max_pages), f32),
@@ -320,11 +308,11 @@
     )(*(in_hbm(x) for x in (lens, owner, slot, q, nk, nv, k, v)))
 
 
-def near_call(got, peers, scale, interpret):
+def near_call(got, peers, interpret):
     sent, dim = got.shape
     block = sent // (4 * NEAR) * 3 + 2
     return pl.pallas_call(
-        lambda *refs: near_kernel(*refs, scale=scale),
+        near_kernel,
         out_shape=jax.ShapeDtypeStruct((peers * block, dim), bf16),
         in_specs=[VMEM],
         out_specs=VMEM,
@@ -334,10 +322,10 @@
     )(got)
 
 
-def project_call(everything, w, mine, block, scale, interpret):
+def project_call(everything, w, mine, block, interpret):
     inner, features = w.shape
     return pl.pallas_call(
-        lambda *refs: project_kernel(*refs, scale=scale, block=block),
+        lambda *refs: project_kernel(*refs, block=block),
         out_shape=jax.ShapeDtypeStruct((mine, features), bf16),
         in_specs=[VMEM, VMEM],
         out_specs=VMEM,

time: 61.3 us -> 60 us (0.979)
  Pallas kernels: 8.34 us -> 6.98 us
    pallas_call x1, Pallas kernels: 6.68 us -> 5.33 us  [attend_call(): pl.pallas_call(lambda *refs: attend_kernel(*refs, position=position), out...]
where the time goes in v4:
time: 60 us; the launch traced here: 59.8 us
  blocking collectives  52.8 us (88%)
  Pallas kernels  6.98 us (12%)
    all_to_all x1, blocking collectives, local(): everything = lax.all_to_all(merged, ('far', 'near'), 0, 0, tiled=True)  33.5 us
    all_to_all x1, blocking collectives, local(): got = lax.all_to_all(partial, ('heads', 'near'), 0, 0, tiled=True)  19.3 us
    pallas_call x1, Pallas kernels, attend_call(): pl.pallas_call(lambda *refs: attend_kernel(*refs, position=position), out...  5.33 us
    pallas_call x1, Pallas kernels, project_call(): pl.pallas_call(lambda *refs: project_kernel(*refs, block=block), out_shap...  1.38 us

profile of v4, /device:TPU:40, one launch (start us, length us, event | category | flops | bytes accessed | tf_op | source)
XLA Modules:
  0.0 59.8 jit_solution(8339397662336748362)
XLA Ops:
  0.0 0.0 copy-start
  0.0 5.3 %attend.1 = bf16[128,128]{1,0:T(8,128)(2,1)S(1)} custom-call(s32[16]{0:T(128)} %refs_0_.1, s32[16,1024]{1,0:T(8,128)} %refs_1_.1, s32[16,1024]{1,0:T(8,128)} %refs_2_.1, bf16[96,128]{1,0:T(8,128)(2,1)} %bitcast.17, bf16[16,128]{1,0:T(8,128)(2,1)} %bitcast.18, bf16[16,128]{1,0:T(8,128)(2,1)} %bitcast.19, bf16[16384,128]{1,0:T(8,128)(2,1)} %bitcast.15, ...), custom_call_target="tpu_custom_call" | custom-call | tf_op jit(solution)/shard_map/attend/pallas_call | solution.py:287
  5.3 19.3 %all_to_all.16 = bf16[32,4,128]{2,1,0:T(4,128)(2,1)S(1)} all-to-all(bf16[32,4,128]{2,1,0:T(4,128)(2,1)S(1)} %bitcast.13), channel_id=1, replica_groups=mesh['group'=2,'far'=4,'near'=4,'heads'=8] {'heads','near'}, dimensions={0} | all-to-all | bytes 65536 | tf_op jit(solution)/shard_map/all_to_all | solution.py:269
  24.6 0.3 near.1
  24.9 33.5 %all_to_all.17 = bf16[16,13,2,128]{3,2,1,0:T(2,128)(2,1)S(1)} all-to-all(bf16[16,13,2,128]{3,2,1,0:T(2,128)(2,1)S(1)} %bitcast.11), channel_id=1, replica_groups=mesh['group'=2,'far'=4,'near'=4,'heads'=8] {'far','near'}, dimensions={0} | all-to-all | bytes 212992 | tf_op jit(solution)/shard_map/all_to_all | solution.py:274
  58.4 0.0 copy-done
  58.4 1.4 %project.1 = bf16[2,384]{1,0:T(2,128)(2,1)} custom-call(bf16[416,128]{1,0:T(8,128)(2,1)S(1)} %bitcast.12, bf16[6144,384]{1,0:T(8,128)(2,1)S(1)} %copy-done), custom_call_target="tpu_custom_call" | custom-call | tf_op jit(solution)/shard_map/project/pallas_call | solution.py:327
Async XLA Ops:
  0.0 58.4 %copy-start = (bf16[6144,384]{1,0:T(8,128)(2,1)S(1)}, bf16[6144,384]{1,0:T(8,128)(2,1)}, u32[]{:S(2)}) copy-start(bf16[6144,384]{1,0:T(8,128)(2,1)} %refs_1_.2) | copy-start | bytes 14155780

commit v5 on v4

--- a/solution.py
+++ b/solution.py
@@ -317,6 +317,7 @@
         in_specs=[VMEM],
         out_specs=VMEM,
         compiler_params=pltpu.CompilerParams(vmem_limit_bytes=4 << 20),
+        cost_estimate=pl.CostEstimate(flops=10**13, transcendentals=0, bytes_accessed=0),
         interpret=interpret,
         name="near",
     )(got)

time: 60 us -> 60.1 us (level)
  no operation moved by 1% of the time
where the time goes in v5:
time: 60.1 us; the launch traced here: 59.9 us
  blocking collectives  53.1 us (88%)
  Pallas kernels  6.84 us (11%)
    all_to_all x1, blocking collectives, local(): everything = lax.all_to_all(merged, ('far', 'near'), 0, 0, tiled=True)  33.8 us
    all_to_all x1, blocking collectives, local(): got = lax.all_to_all(partial, ('heads', 'near'), 0, 0, tiled=True)  19.3 us
    pallas_call x1, Pallas kernels, attend_call(): pl.pallas_call(lambda *refs: attend_kernel(*refs, position=position), out...  5.18 us
    pallas_call x1, Pallas kernels, project_call(): pl.pallas_call(lambda *refs: project_kernel(*refs, block=block), out_shap...  1.4 us

profile of v5, /device:TPU:40, one launch (start us, length us, event | category | flops | bytes accessed | tf_op | source)
XLA Modules:
  0.0 59.9 jit_solution(8709867931818547136)
XLA Ops:
  0.0 5.2 %attend.1 = bf16[128,128]{1,0:T(8,128)(2,1)S(1)} custom-call(s32[16]{0:T(128)} %refs_0_.1, s32[16,1024]{1,0:T(8,128)} %refs_1_.1, s32[16,1024]{1,0:T(8,128)} %refs_2_.1, bf16[96,128]{1,0:T(8,128)(2,1)} %bitcast.17, bf16[16,128]{1,0:T(8,128)(2,1)} %bitcast.18, bf16[16,128]{1,0:T(8,128)(2,1)} %bitcast.19, bf16[16384,128]{1,0:T(8,128)(2,1)} %bitcast.15, ...), custom_call_target="tpu_custom_call" | custom-call | tf_op jit(solution)/shard_map/attend/pallas_call | solution.py:287
  5.2 19.3 %all_to_all.16 = bf16[32,4,128]{2,1,0:T(4,128)(2,1)S(1)} all-to-all(bf16[32,4,128]{2,1,0:T(4,128)(2,1)S(1)} %bitcast.12), channel_id=1, replica_groups=mesh['group'=2,'far'=4,'near'=4,'heads'=8] {'heads','near'}, dimensions={0} | all-to-all | bytes 65536 | tf_op jit(solution)/shard_map/all_to_all | solution.py:269
  24.5 0.0 copy-start
  24.5 0.3 near.1
  24.8 33.8 %all_to_all.17 = bf16[16,13,2,128]{3,2,1,0:T(2,128)(2,1)S(1)} all-to-all(bf16[16,13,2,128]{3,2,1,0:T(2,128)(2,1)S(1)} %bitcast.13), channel_id=1, replica_groups=mesh['group'=2,'far'=4,'near'=4,'heads'=8] {'far','near'}, dimensions={0} | all-to-all | bytes 212992 | tf_op jit(solution)/shard_map/all_to_all | solution.py:274
  58.5 0.0 copy-done
  58.5 1.4 %project.1 = bf16[2,384]{1,0:T(2,128)(2,1)} custom-call(bf16[416,128]{1,0:T(8,128)(2,1)S(1)} %bitcast.11, bf16[6144,384]{1,0:T(8,128)(2,1)S(1)} %copy-done), custom_call_target="tpu_custom_call" | custom-call | tf_op jit(solution)/shard_map/project/pallas_call | solution.py:328
Async XLA Ops:
  24.5 34.1 %copy-start = (bf16[6144,384]{1,0:T(8,128)(2,1)S(1)}, bf16[6144,384]{1,0:T(8,128)(2,1)}, u32[]{:S(2)}) copy-start(bf16[6144,384]{1,0:T(8,128)(2,1)} %refs_1_.2) | copy-start | bytes 14155780

commit v6 on v4

--- a/solution.py
+++ b/solution.py
@@ -160,8 +160,10 @@
     source = iota((sent, 2 * rows), 1)
     inner = jnp.where(source < rows, source, source - rows)
     flat = (inner % requests) * heads + inner // requests
-    data = (source < rows) & (to % 4 < 3) & (flat == (to // 4) * 3 + to % 4)
-    head_row = (source >= rows) & (to % 4 == 3) & (flat // 3 == to // 4)
+    peers = sent // (4 * NEAR)
+    third = (to // 4) % peers * NEAR + to // 4 // peers
+    data = (source < rows) & (to % 4 < 3) & (flat == third * 3 + to % 4)
+    head_row = (source >= rows) & (to % 4 == 3) & (flat // 3 == third)
     pick = jnp.where(data, 1.0, jnp.where(head_row, 1.0, 0.0)).astype(bf16)
     out_ref[...] = dot(pick, both).astype(bf16)
 
@@ -177,7 +179,7 @@
     source = iota((height, sent), 1)
     line = to % kept
     near = (to // kept) % NEAR
-    base = (line // 3) * (4 * NEAR) + near * 4
+    base = near * (4 * blocks) + (line // 3) * 4
     wanted = jnp.where(to < NEAR * kept, base + line % 3, base + 3)
     pick = jnp.where((source == wanted) & (line < mine), 1.0, 0.0).astype(bf16)
     all_rows = dot(pick, got)
@@ -266,7 +268,7 @@
         k_cache.reshape(tokens, dim), v_cache.reshape(tokens, dim), sent, interpret,
     )
     partial, out_weight = lax.optimization_barrier((partial, out_weight))
-    got = lax.all_to_all(partial, ("heads", "near"), 0, 0, tiled=True)
+    got = lax.all_to_all(partial, ("near", "heads"), 0, 0, tiled=True)
     peers = lax.axis_size("far") * lax.axis_size("near")
     merged = near_call(got, peers, interpret)
     block = merged.shape[0] // peers

time: 60 us -> 60.3 us (level)
  no operation moved by 1% of the time
where the time goes in v6:
time: 60.3 us; the launch traced here: 60.1 us
  blocking collectives  53.1 us (88%)
  Pallas kernels  6.99 us (12%)
    all_to_all x1, blocking collectives, local(): everything = lax.all_to_all(merged, ('far', 'near'), 0, 0, tiled=True)  33.8 us
    all_to_all x1, blocking collectives, local(): got = lax.all_to_all(partial, ('near', 'heads'), 0, 0, tiled=True)  19.3 us
    pallas_call x1, Pallas kernels, attend_call(): pl.pallas_call(lambda *refs: attend_kernel(*refs, position=position), out...  5.34 us
    pallas_call x1, Pallas kernels, project_call(): pl.pallas_call(lambda *refs: project_kernel(*refs, block=block), out_shap...  1.38 us

profile of v6, /device:TPU:40, one launch (start us, length us, event | category | flops | bytes accessed | tf_op | source)
XLA Modules:
  0.0 60.1 jit_solution(10932635329777918374)
XLA Ops:
  0.0 0.0 copy-start
  0.0 5.3 %attend.1 = bf16[128,128]{1,0:T(8,128)(2,1)S(1)} custom-call(s32[16]{0:T(128)} %refs_0_.1, s32[16,1024]{1,0:T(8,128)} %refs_1_.1, s32[16,1024]{1,0:T(8,128)} %refs_2_.1, bf16[96,128]{1,0:T(8,128)(2,1)} %bitcast.17, bf16[16,128]{1,0:T(8,128)(2,1)} %bitcast.18, bf16[16,128]{1,0:T(8,128)(2,1)} %bitcast.19, bf16[16384,128]{1,0:T(8,128)(2,1)} %bitcast.15, ...), custom_call_target="tpu_custom_call" | custom-call | tf_op jit(solution)/shard_map/attend/pallas_call | solution.py:289
  5.3 19.3 %all_to_all.16 = bf16[32,4,128]{2,1,0:T(4,128)(2,1)S(1)} all-to-all(bf16[32,4,128]{2,1,0:T(4,128)(2,1)S(1)} %bitcast.13), channel_id=1, replica_groups=mesh['group'=2,'far'=4,'near'=4,'heads'=8] {'near','heads'}, dimensions={0} | all-to-all | bytes 65536 | tf_op jit(solution)/shard_map/all_to_all | solution.py:271
  24.7 0.3 near.1
  25.0 33.8 %all_to_all.17 = bf16[16,13,2,128]{3,2,1,0:T(2,128)(2,1)S(1)} all-to-all(bf16[16,13,2,128]{3,2,1,0:T(2,128)(2,1)S(1)} %bitcast.11), channel_id=1, replica_groups=mesh['group'=2,'far'=4,'near'=4,'heads'=8] {'far','near'}, dimensions={0} | all-to-all | bytes 212992 | tf_op jit(solution)/shard_map/all_to_all | solution.py:276
  58.7 0.0 copy-done
  58.7 1.4 %project.1 = bf16[2,384]{1,0:T(2,128)(2,1)} custom-call(bf16[416,128]{1,0:T(8,128)(2,1)S(1)} %bitcast.12, bf16[6144,384]{1,0:T(8,128)(2,1)S(1)} %copy-done), custom_call_target="tpu_custom_call" | custom-call | tf_op jit(solution)/shard_map/project/pallas_call | solution.py:329
Async XLA Ops:
  0.0 58.7 %copy-start = (bf16[6144,384]{1,0:T(8,128)(2,1)S(1)}, bf16[6144,384]{1,0:T(8,128)(2,1)}, u32[]{:S(2)}) copy-start(bf16[6144,384]{1,0:T(8,128)(2,1)} %refs_1_.2) | copy-start | bytes 14155780

commit v7 on v4

--- a/solution.py
+++ b/solution.py
@@ -71,6 +71,16 @@
     for copy in small:
         copy.start()
     order[0].start()
+    lane = iota((rows, 128), 1)
+    group = (iota((rows, 128), 0) // requests) % 3
+    sent = out_ref.shape[0]
+    to = iota((sent, 2 * rows), 0)
+    source = iota((sent, 2 * rows), 1)
+    inner = jnp.where(source < rows, source, source - rows)
+    flat = (inner % requests) * heads + inner // requests
+    data = (source < rows) & (to % 4 < 3) & (flat == (to // 4) * 3 + to % 4)
+    head_row = (source >= rows) & (to % 4 == 3) & (flat // 3 == to // 4)
+    pick = jnp.where(data, 1.0, jnp.where(head_row, 1.0, 0.0)).astype(bf16)
     for copy in small:
         copy.wait()
     for copy in order[1:]:
@@ -149,20 +159,10 @@
     out = out * keep + take * nv
     total = total * keep + take
 
-    lane = iota((rows, 128), 1)
-    group = (iota((rows, 128), 0) // requests) % 3
     meta = jnp.zeros((rows, 128), f32)
     for i, part in enumerate(split3(new_top) + split3(total)):
         meta = jnp.where(lane == 6 * group + i, part, meta)
     both = jnp.concatenate([out.astype(bf16), meta.astype(bf16)], axis=0)
-    sent = out_ref.shape[0]
-    to = iota((sent, 2 * rows), 0)
-    source = iota((sent, 2 * rows), 1)
-    inner = jnp.where(source < rows, source, source - rows)
-    flat = (inner % requests) * heads + inner // requests
-    data = (source < rows) & (to % 4 < 3) & (flat == (to // 4) * 3 + to % 4)
-    head_row = (source >= rows) & (to % 4 == 3) & (flat // 3 == to // 4)
-    pick = jnp.where(data, 1.0, jnp.where(head_row, 1.0, 0.0)).astype(bf16)
     out_ref[...] = dot(pick, both).astype(bf16)
 
 

time: 60 us -> 60 us (level)
  no operation moved by 1% of the time
where the time goes in v7:
time: 60 us; the launch traced here: 59.8 us
  blocking collectives  52.8 us (88%)
  Pallas kernels  6.95 us (12%)
    all_to_all x1, blocking collectives, local(): everything = lax.all_to_all(merged, ('far', 'near'), 0, 0, tiled=True)  33.5 us
    all_to_all x1, blocking collectives, local(): got = lax.all_to_all(partial, ('heads', 'near'), 0, 0, tiled=True)  19.3 us
    pallas_call x1, Pallas kernels, attend_call(): pl.pallas_call(lambda *refs: attend_kernel(*refs, position=position), out...  5.3 us
    pallas_call x1, Pallas kernels, project_call(): pl.pallas_call(lambda *refs: project_kernel(*refs, block=block), out_shap...  1.38 us

profile of v7, /device:TPU:40, one launch (start us, length us, event | category | flops | bytes accessed | tf_op | source)
XLA Modules:
  0.0 59.8 jit_solution(9174168009591699810)
XLA Ops:
  0.0 0.0 copy-start
  0.0 5.3 %attend.1 = bf16[128,128]{1,0:T(8,128)(2,1)S(1)} custom-call(s32[16]{0:T(128)} %refs_0_.1, s32[16,1024]{1,0:T(8,128)} %refs_1_.1, s32[16,1024]{1,0:T(8,128)} %refs_2_.1, bf16[96,128]{1,0:T(8,128)(2,1)} %bitcast.17, bf16[16,128]{1,0:T(8,128)(2,1)} %bitcast.18, bf16[16,128]{1,0:T(8,128)(2,1)} %bitcast.19, bf16[16384,128]{1,0:T(8,128)(2,1)} %bitcast.15, ...), custom_call_target="tpu_custom_call" | custom-call | tf_op jit(solution)/shard_map/attend/pallas_call | solution.py:287
  5.3 19.3 %all_to_all.16 = bf16[32,4,128]{2,1,0:T(4,128)(2,1)S(1)} all-to-all(bf16[32,4,128]{2,1,0:T(4,128)(2,1)S(1)} %bitcast.13), channel_id=1, replica_groups=mesh['group'=2,'far'=4,'near'=4,'heads'=8] {'heads','near'}, dimensions={0} | all-to-all | bytes 65536 | tf_op jit(solution)/shard_map/all_to_all | solution.py:269
  24.6 0.3 near.1
  24.9 33.5 %all_to_all.17 = bf16[16,13,2,128]{3,2,1,0:T(2,128)(2,1)S(1)} all-to-all(bf16[16,13,2,128]{3,2,1,0:T(2,128)(2,1)S(1)} %bitcast.11), channel_id=1, replica_groups=mesh['group'=2,'far'=4,'near'=4,'heads'=8] {'far','near'}, dimensions={0} | all-to-all | bytes 212992 | tf_op jit(solution)/shard_map/all_to_all | solution.py:274
  58.4 0.0 copy-done
  58.4 1.4 %project.1 = bf16[2,384]{1,0:T(2,128)(2,1)} custom-call(bf16[416,128]{1,0:T(8,128)(2,1)S(1)} %bitcast.12, bf16[6144,384]{1,0:T(8,128)(2,1)S(1)} %copy-done), custom_call_target="tpu_custom_call" | custom-call | tf_op jit(solution)/shard_map/project/pallas_call | solution.py:327
Async XLA Ops:
  0.0 58.4 %copy-start = (bf16[6144,384]{1,0:T(8,128)(2,1)S(1)}, bf16[6144,384]{1,0:T(8,128)(2,1)}, u32[]{:S(2)}) copy-start(bf16[6144,384]{1,0:T(8,128)(2,1)} %refs_1_.2) | copy-start | bytes 14155780
